TPU v7x, 32 devices: a whole 2x2x4 slice. The times are simulated.
32 devices in a mesh: leaf: 4 (over x, core), ctx: 8 (over z, y).
Axes of the slice: x: 2, y: 2, z: 4, core: 2. Of those that a mesh axis runs over, the one named last changes fastest.
Arguments:
- queries: bfloat16 [4096, 4096], P(('leaf', 'ctx')), parts along dimension 0, may hold values from -6 to 6
- keys: bfloat16 [4096, 512], P(('leaf', 'ctx')), parts along dimension 0, may hold values from -6 to 6
- values: bfloat16 [4096, 512], P(('leaf', 'ctx')), parts along dimension 0, may hold values from -6 to 6
- grad_out: bfloat16 [4096, 4096], P(('leaf', 'ctx')), parts along dimension 0, may hold values from -6 to 6
- block_path: int32 [32, 4], P('leaf'), parts along dimension 0, may hold values from -1 to 7, as said below
- assistant: int32 [4096], P(('leaf', 'ctx')), parts along dimension 0, may hold values from 0 to 1, as said below
Outputs:
- attention: bfloat16 [4096, 4096], P(('leaf', 'ctx')), parts along dimension 0
- grad_queries: bfloat16 [4096, 4096], P(('leaf', 'ctx')), parts along dimension 0
- grad_keys: bfloat16 [4096, 512], P(('leaf', 'ctx')), parts along dimension 0
- grad_values: bfloat16 [4096, 512], P(('leaf', 'ctx')), parts along dimension 0
There are 4 independent parts, one for each index of `leaf`. A program takes and returns all parts, laid end to end along the dimension named above; each array names one. Nothing has to cross between parts.
Inputs may be any that keep to these rules, and one draw needn't show every extreme that they name: `block_path`: blocks lie in depth-first order of the tree; every node spans one block; block 0 is the root at depth 0. Row b holds at depth e <= depth(b) the block of b's ancestor node at that depth (b itself at e = depth(b)) and -1 below. `assistant`: each block of 128 tokens holds one run of ones.
All inputs are finite; a program needn't handle non-finite values.
Results may differ from a plain program's by a relative error of at most 0.0091.
Values may be sent and summed in bfloat16 or wider, within the bound.
No kernel may reach another device: no remote copies, remote signals or barrier semaphores. Data moves between devices by JAX's collectives and lax.ppermute only.
A program may use at most 128 MiB of HBM per device.

v0:
```python
import math
import jax
import jax.numpy as jnp
from jax import lax
from jax.sharding import PartitionSpec as P

KEY_HEADS = 4
HEAD_WIDTH = 128
HEADS_PER_KEY = 8


def prefix(x, axis, combine, identity):
    size, here = (lax.axis_size(axis), lax.axis_index(axis))
    everything = jax.tree.map(lambda part: lax.all_gather(part, axis), x)
    start = jax.tree.map(
        lambda part, zero: jnp.broadcast_to(jnp.asarray(zero, part.dtype), part.shape), x, identity
    )

    def hop(k, before):
        at = size - 1 - k
        reached = at > here
        new = combine(before, jax.tree.map(lambda part: part[at], everything))
        return jax.tree.map(lambda a, b: jnp.where(reached, a, b), new, before)

    return lax.fori_loop(0, size, hop, start)


def dot_rows(left, right):
    return lax.dot_general(
        left, right, (((1,), (1,)), ((), ())), preferred_element_type=jnp.float32
    )


def dot_cols(left, right):
    return lax.dot_general(
        left, right, (((0,), (0,)), ((), ())), preferred_element_type=jnp.float32
    )


def attend_block(queries, grad_rows, slot_keys, slot_values, allowed):
    block_rows = queries.shape[0]
    head_cols = HEADS_PER_KEY * HEAD_WIDTH
    scaling = 1.0 / math.sqrt(HEAD_WIDTH)
    wide_mask = jnp.repeat(allowed, HEADS_PER_KEY, axis=0)
    attended_parts, query_parts, key_parts, value_parts = ([], [], [], [])
    for key_value_head in range(KEY_HEADS):
        query_matrix = queries[
            :, key_value_head * head_cols : (key_value_head + 1) * head_cols
        ].reshape(block_rows * HEADS_PER_KEY, HEAD_WIDTH)
        grad_head = grad_rows[
            :, key_value_head * head_cols : (key_value_head + 1) * head_cols
        ].reshape(block_rows * HEADS_PER_KEY, HEAD_WIDTH)
        key_cols = slot_keys[:, key_value_head * HEAD_WIDTH : (key_value_head + 1) * HEAD_WIDTH]
        value_cols = slot_values[:, key_value_head * HEAD_WIDTH : (key_value_head + 1) * HEAD_WIDTH]
        scores = jnp.where(wide_mask, dot_rows(query_matrix, key_cols) * scaling, -jnp.inf)
        row_max = jnp.max(scores, axis=1, keepdims=True)
        row_sum = jnp.sum(jnp.exp(scores - row_max), axis=1, keepdims=True)
        log_total = row_max + jnp.log(row_sum)
        rounded = jnp.exp(scores - log_total).astype(jnp.bfloat16)
        attended = jnp.dot(rounded, value_cols, preferred_element_type=jnp.float32).astype(
            jnp.bfloat16
        )
        attended = lax.optimization_barrier(attended)
        row_delta = jnp.sum(
            grad_head.astype(jnp.float32) * attended.astype(jnp.float32), axis=1, keepdims=True
        )
        grad_prob = dot_rows(grad_head, value_cols)
        grad_score = (jnp.exp(scores - log_total) * (grad_prob - row_delta)).astype(jnp.bfloat16)
        grad_query = (
            jnp.dot(grad_score, key_cols, preferred_element_type=jnp.float32) * scaling
        ).astype(jnp.bfloat16)
        grad_key = dot_cols(grad_score, query_matrix) * scaling
        grad_value = dot_cols(rounded, grad_head)
        attended_parts.append(attended.reshape(block_rows, head_cols))
        query_parts.append(grad_query.reshape(block_rows, head_cols))
        key_parts.append(grad_key)
        value_parts.append(grad_value)
    return (
        jnp.concatenate(attended_parts, 1),
        jnp.concatenate(query_parts, 1),
        jnp.concatenate(key_parts, 1),
        jnp.concatenate(value_parts, 1),
    )


def on_device(queries, keys, values, grad_out, block_path, assistant):
    block_rows = queries.shape[0]
    kv_width = keys.shape[1]
    position = lax.axis_index("ctx")
    depths = jnp.sum((block_path >= 0).astype(jnp.int32), axis=1) - 1
    own_path = lax.dynamic_index_in_dim(block_path, position, 0, keepdims=False)
    own_depth = lax.dynamic_index_in_dim(depths, position, 0, keepdims=False)
    seen_slots = jnp.stack([own_depth > 0, own_depth > 1, own_depth > 2])
    wanted_blocks = jnp.stack([own_path[0], own_path[1], own_path[2]])
    row_ids = jnp.arange(block_rows, dtype=jnp.int32)
    empty = jnp.zeros((3, block_rows, kv_width), jnp.bfloat16)
    picked = (empty, empty)
    key_piece = lax.all_gather(keys, "ctx", axis=0, tiled=True)
    value_piece = lax.all_gather(values, "ctx", axis=0, tiled=True)
    piece_rows = key_piece.shape[0]
    for slot_number in range(3):
        wanted = wanted_blocks[slot_number]
        begin = wanted * block_rows
        touches = (wanted >= 0) & (begin < piece_rows) & (begin + block_rows > 0)

        def fill(current, slot_number=slot_number, begin=begin):
            local_rows = begin + row_ids
            inside = (local_rows >= 0) & (local_rows < piece_rows)
            clipped = jnp.clip(local_rows, 0, piece_rows - 1)
            new_keys = jnp.where(inside[:, None], key_piece[clipped], current[0][slot_number])
            new_values = jnp.where(inside[:, None], value_piece[clipped], current[1][slot_number])
            return (
                current[0].at[slot_number].set(new_keys),
                current[1].at[slot_number].set(new_values),
            )

        def unchanged(current):
            return current

        picked = lax.cond(touches, fill, unchanged, picked)
    far_keys, far_values = picked
    slot_keys = jnp.concatenate([far_keys.reshape(3 * block_rows, kv_width), keys], 0)
    slot_values = jnp.concatenate([far_values.reshape(3 * block_rows, kv_width), values], 0)
    full_slots = jnp.repeat(seen_slots, block_rows)
    causal = jnp.arange(block_rows)[:, None] >= jnp.arange(block_rows)[None, :]
    allowed = jnp.concatenate(
        [jnp.broadcast_to(full_slots[None, :], (block_rows, 3 * block_rows)), causal], 1
    )
    grad_rows = grad_out * assistant[:, None].astype(jnp.bfloat16)
    attention, grad_queries, grad_key_all, grad_value_all = attend_block(
        queries, grad_rows, slot_keys, slot_values, allowed
    )
    slot_grads = jnp.stack(
        [
            grad_key_all.reshape(4, block_rows, kv_width),
            grad_value_all.reshape(4, block_rows, kv_width),
        ],
        1,
    )
    grad_total = slot_grads[3]
    tree_depths = [0, 1, 2]
    resets = jnp.stack([own_depth <= tree_level for tree_level in tree_depths]).astype(jnp.float32)
    carried = jnp.stack([slot_grads[tree_level] for tree_level in tree_depths])

    def accumulate(earlier, latter):
        marker = jnp.maximum(earlier[0], latter[0])
        summed = jnp.where(latter[0][:, None, None, None] > 0.5, latter[1], earlier[1] + latter[1])
        return (marker, summed)

    identity = (jnp.zeros_like(resets), jnp.zeros_like(carried))
    _, received = prefix((resets, carried), "ctx", accumulate, identity)
    for slot_index, tree_level in enumerate(tree_depths):
        grad_total = grad_total + jnp.where(own_depth == tree_level, received[slot_index], 0.0)
    return (
        attention,
        grad_queries,
        grad_total[0].astype(jnp.bfloat16),
        grad_total[1].astype(jnp.bfloat16),
    )


def solution(mesh):
    in_specs = (
        P(("leaf", "ctx"), None),
        P(("leaf", "ctx"), None),
        P(("leaf", "ctx"), None),
        P(("leaf", "ctx"), None),
        P("leaf", None),
        P(("leaf", "ctx")),
    )
    out_specs = (
        P(("leaf", "ctx"), None),
        P(("leaf", "ctx"), None),
        P(("leaf", "ctx"), None),
        P(("leaf", "ctx"), None),
    )
    return jax.shard_map(
        on_device, mesh=mesh, in_specs=in_specs, out_specs=out_specs, check_vma=False
    )
```

profile of v0, /device:TPU:0, one launch (start us, length us, event | category | flops | bytes accessed | tf_op | source)
XLA Modules:
  0.0 329.6 jit_solution(16792930033362038903)
XLA Ops:
  19.0 1.1 reshape.481
  23.4 29.8 %all-gather.6.cloned.1.call-done = bf16[1024,512]{1,0:T(8,128)(2,1)} async-done(((bf16[128,512]{1,0:T(8,128)(2,1)}), bf16[1024,512]{1,0:T(8,128)(2,1)}) %all-gather.6.cloned.1.call-update) | async-done | bytes 1048592 | tf_op jit(solution)/shard_map/all_gather | solution.py:98
  53.2 41.1 %all-gather.8.cloned.1.call-done = bf16[1024,512]{1,0:T(8,128)(2,1)} async-done(((bf16[128,512]{1,0:T(8,128)(2,1)}), bf16[1024,512]{1,0:T(8,128)(2,1)}) %all-gather.8.cloned.1.call-update) | async-done | bytes 1048592 | tf_op jit(solution)/shard_map/all_gather | solution.py:99
  94.3 4.7 %conditional.3 = (bf16[3,128,512]{2,1,0:T(8,128)(2,1)S(1)}, bf16[3,128,512]{2,1,0:T(8,128)(2,1)S(1)}) conditional(s32[]{:T(128)} %convert_element_type.109, () %tuple.88, (s32[]{:T(128)}, s32[128]{0:T(128)S(1)}, bf16[1024,512]{1,0:T(8,128)(2,1)}, bf16[1024,512]{1,0:T(8,128)(2,1)}) %tuple.89), branch_computations={%region_1.2_spmd, %region_2.3_spmd} | conditional | flops 133248 | bytes 2104604 | solution.py:120
  94.3 2.2 gather_fusion.1
  96.6 2.2 gather_fusion
  109.2 1.5 multiply_convert_fusion.2
  111.4 1.5 multiply_convert_fusion.3
  113.0 1.1 pad_maximum_fusion.4
  114.0 1.6 copy.47
  116.2 1.7 convolution_multiply_fusion.5
  119.3 1.3 pad_maximum_fusion
  122.8 24.4 %all-gather.1 = f32[8,1,3]{2,1,0:T(1,128)S(1)} all-gather(f32[1,1,3]{2,1,0:T(1,128)S(1)} %fusion.44), channel_id=1, replica_groups=mesh['leaf'=4,'ctx'=8] {'ctx'}, dimensions={0}, use_global_device_ids=true | all-gather | bytes 108 | tf_op jit(solution)/shard_map/all_gather | solution.py:14
  150.0 1.8 reshape.480
  151.8 1.8 reshape.478
  153.5 1.8 reshape.476
  155.3 1.7 fusion.12
  157.8 1.7 fusion.11
  160.4 1.7 fusion.10
  162.9 1.7 fusion.9
  165.5 2.3 pad_maximum_fusion.1
  168.9 135.4 %all-gather.10.cloned.1.call-done = f32[24,2,128,512]{3,2,1,0:T(8,128)} async-done(((f32[3,2,128,512]{3,2,1,0:T(8,128)}), f32[24,2,128,512]{3,2,1,0:T(8,128)}) %all-gather.10.cloned.1.call-update) | async-done | bytes 12582928 | tf_op jit(solution)/shard_map/all_gather | solution.py:14
  304.3 16.8 %while.22 = (s32[]{:T(128)}, f32[3,2,128,512]{3,2,1,0:T(8,128)S(1)}, s32[]{:T(128)}, f32[8,3]{1,0:T(8,128)S(1)}, f32[8,3,2,128,512]{4,3,2,1,0:T(8,128)}, /*index=5*/s32[]{:T(128)}, s32[]{:T(128)}, s32[]{:T(128)}, s32[]{:T(128)}) while((s32[]{:T(128)}, f32[3,2,128,512]{3,2,1,0:T(8,128)S(1)}, s32[]{:T(128)}, ...), condition=%wide.region_20.21_spmd.clone, body=%wide.region_19.20_spmd.clone.sunk | while | flops 1572875 | bytes 4718785 | solution.py:25
  304.3 2.0 fusion.77
  306.4 2.1 fusion.77
  308.5 2.1 fusion.77
  310.6 2.1 fusion.77
  312.8 2.1 fusion.77
  314.9 2.1 fusion.77
  317.0 2.1 fusion.77
  319.1 2.1 fusion.77
  321.1 1.2 fusion.15
  (147 shorter events, 28.0 us)
Async XLA Ops:
  7.2 11.1 %copy-start.20 = (bf16[128,4096]{1,0:T(8,128)(2,1)S(1)}, bf16[128,4096]{1,0:T(8,128)(2,1)}, u32[]{:S(2)}) copy-start(bf16[128,4096]{1,0:T(8,128)(2,1)} %param.26) | copy-start | bytes 3145732
  7.2 46.0 %all-gather.6.cloned.1.call-start = ((), (), s32[]{:S(2)}) async-start(), calls=%async_computation | async-start | bytes 1179648 | tf_op jit(solution)/shard_map/all_gather | solution.py:98
  7.9 86.4 %all-gather.8.cloned.1.call-start = ((), (), s32[]{:S(2)}) async-start(), calls=%async_computation.1 | async-start | bytes 1179648 | tf_op jit(solution)/shard_map/all_gather | solution.py:99
  8.7 295.7 %all-gather.10.cloned.1.call-start = ((), (), s32[]{:S(2)}) async-start(), calls=%async_computation.2 | async-start | bytes 14155776 | tf_op jit(solution)/shard_map/all_gather | solution.py:14
  18.2 4.4 %copy-start.27 = (s32[128]{0:T(128)S(1)}, s32[128]{0:T(128)}, u32[]{:S(2)}) copy-start(s32[128]{0:T(128)} %param.31) | copy-start | bytes 1540
  18.2 4.4 %copy-start.19 = (bf16[128,4096]{1,0:T(8,128)(2,1)S(1)}, bf16[128,4096]{1,0:T(8,128)(2,1)}, u32[]{:S(2)}) copy-start(bf16[128,4096]{1,0:T(8,128)(2,1)} %param.29) | copy-start | bytes 3145732
  20.1 79.8 %copy-start.12 = (bf16[1024,128]{1,0:T(8,128)(2,1)}, bf16[1024,128]{1,0:T(8,128)(2,1)S(1)}, u32[]{:S(2)}) copy-start(bf16[1024,128]{1,0:T(8,128)(2,1)S(1)} %reshape.481) | copy-start | bytes 786436
  99.0 0.9 copy-start.25
  100.0 4.5 %copy-start.5 = (bf16[512,512]{1,0:T(8,128)(2,1)}, bf16[512,512]{1,0:T(8,128)(2,1)S(1)}, u32[]{:S(2)}) copy-start(bf16[512,512]{1,0:T(8,128)(2,1)S(1)} %constant_dynamic-update-slice_fusion) | copy-start | bytes 1572868
  100.0 1.0 copy-start.26
  100.5 1.1 copy-start.14
  101.6 4.9 %copy-start.7 = (bf16[1024,128]{1,0:T(8,128)(2,1)}, bf16[1024,128]{1,0:T(8,128)(2,1)S(1)}, u32[]{:S(2)}) copy-start(bf16[1024,128]{1,0:T(8,128)(2,1)S(1)} %convolution_convert_fusion) | copy-start | bytes 786436
  102.1 1.0 copy-start.15
  103.1 4.7 %copy-start.9 = (bf16[1024,128]{1,0:T(8,128)(2,1)}, bf16[1024,128]{1,0:T(8,128)(2,1)S(1)}, u32[]{:S(2)}) copy-start(bf16[1024,128]{1,0:T(8,128)(2,1)S(1)} %convolution_convert_fusion.1) | copy-start | bytes 786436
  103.6 1.0 copy-start.17
  104.5 4.5 %copy-start.10 = (bf16[1024,128]{1,0:T(8,128)(2,1)}, bf16[1024,128]{1,0:T(8,128)(2,1)S(1)}, u32[]{:S(2)}) copy-start(bf16[1024,128]{1,0:T(8,128)(2,1)S(1)} %convolution_convert_fusion.2) | copy-start | bytes 786436
  105.9 5.3 %copy-start.11 = (bf16[1024,128]{1,0:T(8,128)(2,1)}, bf16[1024,128]{1,0:T(8,128)(2,1)S(1)}, u32[]{:S(2)}) copy-start(bf16[1024,128]{1,0:T(8,128)(2,1)S(1)} %convolution_convert_fusion.3) | copy-start | bytes 786436
  107.2 8.4 %copy-start.1 = (bf16[1024,512]{0,1:T(8,128)(2,1)}, bf16[1024,512]{0,1:T(8,128)(2,1)S(1)}, u32[]{:S(2)}) copy-start(bf16[1024,512]{0,1:T(8,128)(2,1)S(1)} %multiply_convert_fusion) | copy-start | bytes 3145732
  108.5 7.7 %copy-start.2 = (bf16[1024,512]{0,1:T(8,128)(2,1)}, bf16[1024,512]{0,1:T(8,128)(2,1)S(1)}, u32[]{:S(2)}) copy-start(bf16[1024,512]{0,1:T(8,128)(2,1)S(1)} %multiply_convert_fusion.1) | copy-start | bytes 3145732
  113.0 2.6 copy-start.13
  115.6 2.2 copy-start.3
  115.6 2.2 copy-start.16
  115.6 2.7 copy-start.4
  115.6 2.7 copy-start.18
  119.3 1.5 copy-start
  119.3 29.8 %copy-start.8 = (bf16[1024,128]{1,0:T(8,128)(2,1)S(1)}, bf16[1024,128]{1,0:T(8,128)(2,1)}, u32[]{:S(2)}) copy-start(bf16[1024,128]{1,0:T(8,128)(2,1)} %copy-done.7) | copy-start | bytes 786436
  120.6 34.7 %copy-start.6 = (bf16[512,512]{1,0:T(8,128)(2,1)S(1)}, bf16[512,512]{1,0:T(8,128)(2,1)}, u32[]{:S(2)}) copy-start(bf16[512,512]{1,0:T(8,128)(2,1)} %copy-done.5) | copy-start | bytes 1572868
  164.6 3.2 copy-start.21
  164.7 3.2 copy-start.22
  165.5 2.3 copy-start.23
  165.5 2.3 copy-start.24
Sparse Core Ops, SparseCore 0:
  10.1 43.0 all-gather.5
  55.3 38.9 all-gather.7
  120.7 183.5 all-gather.9
where the time goes:
time: 331 us; the launch traced here: 330 us
  waiting for transfers between devices  208 us (63%)
  other arithmetic  26.8 us (8%)
  local copies, waits for them, and re-layouts  25.5 us (8%)
  blocking collectives  24.4 us (7%)
  between operations  24.2 us (7%)
  matrix products  20.2 us (6%)
    all_gather x1, waiting for transfers between devices, prefix(): everything = jax.tree.map(lambda part: lax.all_gather(part, axis), x)  135 us
    all_gather x1, waiting for transfers between devices, on_device(): value_piece = lax.all_gather(values, 'ctx', axis=0, tiled=True)  41.1 us
    all_gather x1, waiting for transfers between devices, on_device(): key_piece = lax.all_gather(keys, 'ctx', axis=0, tiled=True)  29.8 us
    all_gather x1, blocking collectives, prefix(): everything = jax.tree.map(lambda part: lax.all_gather(part, axis), x)  24.4 us
    select_n x8, other arithmetic, hop(): return jax.tree.map(lambda a, b: jnp.where(reached, a, b), new, before)  16.4 us
    dot_general x4, matrix products, attend_block(): jnp.dot(grad_score, key_cols, preferred_element_type=jnp.float32) * scaling  6.85 us
  transfers between devices with their start and end apart: 3, of which 3 were waited for; matrix products, arithmetic and copies ran while one was open for 9% of the time, Pallas kernels for 0%

commit v1 on v0

--- a/solution.py
+++ b/solution.py
@@ -95,8 +95,11 @@
     row_ids = jnp.arange(block_rows, dtype=jnp.int32)
     empty = jnp.zeros((3, block_rows, kv_width), jnp.bfloat16)
     picked = (empty, empty)
-    key_piece = lax.all_gather(keys, "ctx", axis=0, tiled=True)
-    value_piece = lax.all_gather(values, "ctx", axis=0, tiled=True)
+    key_piece, value_piece = jnp.split(
+        lax.all_gather(jnp.concatenate([keys, values], axis=1), "ctx", axis=0, tiled=True),
+        [keys.shape[1]],
+        axis=1,
+    )
     piece_rows = key_piece.shape[0]
     for slot_number in range(3):
         wanted = wanted_blocks[slot_number]

time: 331 us -> 303 us (0.915)
  waiting for transfers between devices: 208 us -> 172 us
  local copies, waits for them, and re-layouts: 25.5 us -> 29.2 us
    all_gather x2 -> x1, waiting for transfers between devices: 70.9 us -> 37.5 us  [on_device(): lax.all_gather(jnp.concatenate([keys, values], axis=1), 'ctx', axis=0, ti...]
  transfers between devices with their start and end apart: 3 -> 2, of which waited for: 3 -> 2; matrix products, arithmetic and copies ran while one was open for 9% -> 10% of each run, Pallas kernels for 0% -> 0%
where the time goes in v1:
time: 303 us; the launch traced here: 302 us
  waiting for transfers between devices  172 us (57%)
  other arithmetic  29.5 us (10%)
  local copies, waits for them, and re-layouts  29.2 us (10%)
  blocking collectives  24.7 us (8%)
  between operations  24.2 us (8%)
  matrix products  22.4 us (7%)
    all_gather x1, waiting for transfers between devices, prefix(): everything = jax.tree.map(lambda part: lax.all_gather(part, axis), x)  134 us
    all_gather x1, waiting for transfers between devices, on_device(): lax.all_gather(jnp.concatenate([keys, values], axis=1), 'ctx', axis=0, ti...  37.5 us
    all_gather x1, blocking collectives, prefix(): everything = jax.tree.map(lambda part: lax.all_gather(part, axis), x)  24.7 us
    select_n x8, other arithmetic, hop(): return jax.tree.map(lambda a, b: jnp.where(reached, a, b), new, before)  16.4 us
    dot_general x8, matrix products, dot_rows(): lax.dot_general(left, right, (((1,), (1,)), ((), ())), preferred_element_...  8.22 us
    dot_general x4, matrix products, attend_block(): jnp.dot(grad_score, key_cols, preferred_element_type=jnp.float32) * scaling  6.84 us
    reshape x4, local copies, waits for them, and re-layouts, attend_block(): attended_parts.append(attended.reshape(block_rows, head_cols))  6.14 us
  transfers between devices with their start and end apart: 2, of which 2 were waited for; matrix products, arithmetic and copies ran while one was open for 10% of the time, Pallas kernels for 0%

profile of v1, /device:TPU:0, one launch (start us, length us, event | category | flops | bytes accessed | tf_op | source)
XLA Modules:
  0.0 302.1 jit_solution(12920096300468474601)
XLA Ops:
  7.2 1.8 pad_maximum_fusion.5
  19.3 1.8 reshape.481
  25.0 37.5 %all-gather.5.cloned.1.call-done = bf16[1024,1024]{1,0:T(8,128)(2,1)} async-done(((bf16[128,1024]{1,0:T(8,128)(2,1)}), bf16[1024,1024]{1,0:T(8,128)(2,1)}) %all-gather.5.cloned.1.call-update) | async-done | bytes 2097168 | tf_op jit(solution)/shard_map/all_gather | solution.py:99
  62.5 1.7 fusion.45
  64.2 5.0 %conditional.3 = (bf16[3,128,512]{2,1,0:T(8,128)(2,1)}, bf16[3,128,512]{2,1,0:T(8,128)(2,1)}) conditional(s32[]{:T(128)} %convert_element_type.109, () %tuple.88, (s32[]{:T(128)}, s32[128]{0:T(128)S(1)}, bf16[1024,512]{1,0:T(8,128)(2,1)S(1)}, bf16[1024,512]{1,0:T(8,128)(2,1)S(1)}) %tuple.89), branch_computations={%region_1.2_spmd, %region_2.3_spmd} | conditional | flops 133248 | bytes 2104604 | solution.py:123
  65.1 1.5 gather_fusion
  71.3 1.7 fusion.49
  80.3 1.5 multiply_convert_fusion.1
  82.5 1.5 multiply_convert_fusion.2
  84.8 1.5 multiply_convert_fusion.3
  87.4 1.6 copy.47
  89.5 1.7 convolution_multiply_fusion.5
  92.6 1.3 pad_maximum_fusion
  96.1 24.7 %all-gather.1 = f32[8,1,3]{2,1,0:T(1,128)S(1)} all-gather(f32[1,1,3]{2,1,0:T(1,128)S(1)} %fusion.44), channel_id=1, replica_groups=mesh['leaf'=4,'ctx'=8] {'ctx'}, dimensions={0}, use_global_device_ids=true | all-gather | bytes 108 | tf_op jit(solution)/shard_map/all_gather | solution.py:14
  123.5 1.8 reshape.480
  125.3 1.8 reshape.478
  127.1 1.8 reshape.476
  128.9 1.7 fusion.12
  131.4 1.7 fusion.11
  133.9 1.7 fusion.10
  136.5 1.7 fusion.9
  139.1 2.3 pad_maximum_fusion.1
  142.4 134.1 %all-gather.7.cloned.1.call-done = f32[24,2,128,512]{3,2,1,0:T(8,128)} async-done(((f32[3,2,128,512]{3,2,1,0:T(8,128)}), f32[24,2,128,512]{3,2,1,0:T(8,128)}) %all-gather.7.cloned.1.call-update) | async-done | bytes 12582928 | tf_op jit(solution)/shard_map/all_gather | solution.py:14
  276.6 16.8 %while.22 = (s32[]{:T(128)}, f32[3,2,128,512]{3,2,1,0:T(8,128)S(1)}, s32[]{:T(128)}, f32[8,3]{1,0:T(8,128)S(1)}, f32[8,3,2,128,512]{4,3,2,1,0:T(8,128)}, /*index=5*/s32[]{:T(128)}, s32[]{:T(128)}, s32[]{:T(128)}, s32[]{:T(128)}) while((s32[]{:T(128)}, f32[3,2,128,512]{3,2,1,0:T(8,128)S(1)}, s32[]{:T(128)}, ...), condition=%wide.region_20.21_spmd.clone, body=%wide.region_19.20_spmd.clone.sunk | while | flops 1572875 | bytes 4718785 | solution.py:25
  276.6 2.0 fusion.78
  278.7 2.1 fusion.78
  280.8 2.1 fusion.78
  282.9 2.1 fusion.78
  285.0 2.1 fusion.78
  287.1 2.1 fusion.78
  289.2 2.1 fusion.78
  291.3 2.1 fusion.78
  (146 shorter events, 32.9 us)
Async XLA Ops:
  7.2 11.3 %copy-start.21 = (bf16[128,4096]{1,0:T(8,128)(2,1)S(1)}, bf16[128,4096]{1,0:T(8,128)(2,1)}, u32[]{:S(2)}) copy-start(bf16[128,4096]{1,0:T(8,128)(2,1)} %param.26) | copy-start | bytes 3145732
  7.2 55.3 %all-gather.5.cloned.1.call-start = ((), (), s32[]{:S(2)}) async-start(), calls=%async_computation | async-start | bytes 2359296 | tf_op jit(solution)/shard_map/all_gather | solution.py:99
  9.0 267.5 %all-gather.7.cloned.1.call-start = ((), (), s32[]{:S(2)}) async-start(), calls=%async_computation.1 | async-start | bytes 14155776 | tf_op jit(solution)/shard_map/all_gather | solution.py:14
  18.5 5.1 %copy-start.27 = (s32[128]{0:T(128)S(1)}, s32[128]{0:T(128)}, u32[]{:S(2)}) copy-start(s32[128]{0:T(128)} %param.31) | copy-start | bytes 1540
  18.5 5.1 %copy-start.20 = (bf16[128,4096]{1,0:T(8,128)(2,1)S(1)}, bf16[128,4096]{1,0:T(8,128)(2,1)}, u32[]{:S(2)}) copy-start(bf16[128,4096]{1,0:T(8,128)(2,1)} %param.29) | copy-start | bytes 3145732
  24.1 56.0 %copy-start.6 = (bf16[1024,128]{1,0:T(8,128)(2,1)}, bf16[1024,128]{1,0:T(8,128)(2,1)S(1)}, u32[]{:S(2)}) copy-start(bf16[1024,128]{1,0:T(8,128)(2,1)S(1)} %reshape.487) | copy-start | bytes 786436
  71.3 5.5 %copy-start.7 = (bf16[512,512]{1,0:T(8,128)(2,1)}, bf16[512,512]{1,0:T(8,128)(2,1)S(1)}, u32[]{:S(2)}) copy-start(bf16[512,512]{1,0:T(8,128)(2,1)S(1)} %constant_dynamic-update-slice_fusion) | copy-start | bytes 1572868
  71.3 2.0 copy-start.26
  73.0 1.0 copy-start.15
  73.9 4.9 %copy-start.9 = (bf16[1024,128]{1,0:T(8,128)(2,1)}, bf16[1024,128]{1,0:T(8,128)(2,1)S(1)}, u32[]{:S(2)}) copy-start(bf16[1024,128]{1,0:T(8,128)(2,1)S(1)} %convolution_convert_fusion) | copy-start | bytes 786436
  74.4 1.0 copy-start.16
  75.4 4.7 %copy-start.11 = (bf16[1024,128]{1,0:T(8,128)(2,1)}, bf16[1024,128]{1,0:T(8,128)(2,1)S(1)}, u32[]{:S(2)}) copy-start(bf16[1024,128]{1,0:T(8,128)(2,1)S(1)} %convolution_convert_fusion.1) | copy-start | bytes 786436
  75.9 1.0 copy-start.18
  76.9 5.5 %copy-start.12 = (bf16[1024,128]{1,0:T(8,128)(2,1)}, bf16[1024,128]{1,0:T(8,128)(2,1)S(1)}, u32[]{:S(2)}) copy-start(bf16[1024,128]{1,0:T(8,128)(2,1)S(1)} %convolution_convert_fusion.2) | copy-start | bytes 786436
  78.3 6.3 %copy-start.13 = (bf16[1024,128]{1,0:T(8,128)(2,1)}, bf16[1024,128]{1,0:T(8,128)(2,1)S(1)}, u32[]{:S(2)}) copy-start(bf16[1024,128]{1,0:T(8,128)(2,1)S(1)} %convolution_convert_fusion.3) | copy-start | bytes 786436
  79.5 9.4 %copy-start.1 = (bf16[1024,512]{0,1:T(8,128)(2,1)}, bf16[1024,512]{0,1:T(8,128)(2,1)S(1)}, u32[]{:S(2)}) copy-start(bf16[1024,512]{0,1:T(8,128)(2,1)S(1)} %multiply_convert_fusion) | copy-start | bytes 3145732
  80.1 1.7 copy-start.5
  81.8 7.7 %copy-start.2 = (bf16[1024,512]{0,1:T(8,128)(2,1)}, bf16[1024,512]{0,1:T(8,128)(2,1)S(1)}, u32[]{:S(2)}) copy-start(bf16[1024,512]{0,1:T(8,128)(2,1)S(1)} %multiply_convert_fusion.1) | copy-start | bytes 3145732
  86.3 2.6 copy-start.14
  88.9 2.2 copy-start.3
  89.0 2.2 copy-start.17
  89.0 2.7 copy-start.4
  89.0 2.7 copy-start.19
  92.6 1.5 copy-start
  92.6 30.1 %copy-start.10 = (bf16[1024,128]{1,0:T(8,128)(2,1)S(1)}, bf16[1024,128]{1,0:T(8,128)(2,1)}, u32[]{:S(2)}) copy-start(bf16[1024,128]{1,0:T(8,128)(2,1)} %copy-done.9) | copy-start | bytes 786436
  93.9 34.9 %copy-start.8 = (bf16[512,512]{1,0:T(8,128)(2,1)S(1)}, bf16[512,512]{1,0:T(8,128)(2,1)}, u32[]{:S(2)}) copy-start(bf16[512,512]{1,0:T(8,128)(2,1)} %copy-done.7) | copy-start | bytes 1572868
  138.2 3.2 %copy-start.22 = (bf16[128,1024]{1,0:T(8,128)(2,1)S(1)}, bf16[128,1024]{1,0:T(8,128)(2,1)}, u32[]{:S(2)}) copy-start(bf16[128,1024]{1,0:T(8,128)(2,1)} %reshape.490) | copy-start | bytes 786436
  138.2 3.1 %copy-start.23 = (bf16[128,1024]{1,0:T(8,128)(2,1)S(1)}, bf16[128,1024]{1,0:T(8,128)(2,1)}, u32[]{:S(2)}) copy-start(bf16[128,1024]{1,0:T(8,128)(2,1)} %reshape.488) | copy-start | bytes 786436
  139.1 2.3 copy-start.24
  139.1 2.3 copy-start.25
Sparse Core Ops, SparseCore 0:
  10.7 51.7 all-gather.4
  94.1 182.4 all-gather.6
